TPU v7x, 256 devices: a whole 4x4x8 slice. The times are simulated.
256 devices in a mesh: row: 8 (over y, core), col: 32 (over x, z).
Axes of the slice: x: 4, y: 4, z: 8, core: 2. Of those that a mesh axis runs over, the one named last changes fastest.
Arguments:
- phases: int32 [8, 32, 8, 24, 576], P('row', 'col'), may hold values from 0 to 2
- grain: float32 [8, 32, 8, 24, 576], P('row', 'col'), may hold values from 0.5 to 2
- phase_cond: float32 [3], replicated, may hold values from 0.3 to 3
- micro_counts: int32 [8, 32, 8], P('row', 'col'), may hold values from 6 to 12, as said below
- current: float32 [8, 32, 8], P('row', 'col'), may hold values from -5 to 5
- load: float32 [8, 32, 8], P('row', 'col'), may hold values from -16 to 16
Outputs:
- states: float32 [8, 32, 8, 3, 24, 576], P('row', 'col')
- tangent: float32 [8, 32, 8, 3, 3], P('row', 'col')
- increment: float32 [8, 32, 8], P('row', 'col')
- residual: float32 [8, 32, 8], P('row', 'col')
Inputs may be any that keep to these rules, and one draw needn't show every extreme that they name: `micro_counts`: every draw has an element with 12 inner iterations and one with 6.
All inputs are finite; a program needn't handle non-finite values.
Results may differ from a plain program's by a relative error of at most 0.0003.
Values sent between devices are 32-bit elements; how exact they have to be, the bound alone decides.
A program may use at most 64 MiB of HBM per device.

v0:
```python
import functools

import jax
import jax.numpy as jnp
from jax import lax
from jax.experimental import pallas as pl
from jax.experimental.pallas import tpu as pltpu
from jax.sharding import PartitionSpec as P

VOX = 24
YZ = 576
PHASES = 3
MACRO_ITERS = 8

XC, YC, ZC = 3, 12, 3
ELEMENTS = 8
HALF = YZ // 2
SPANS = ((0, 128), (128, 128), (256, 32))


def swap_half(value):
    lane = lax.broadcasted_iota(jnp.int32, value.shape, 1)
    return jnp.where((lane & 8) == 0, pltpu.roll(value, 120, 1), pltpu.roll(value, 8, 1))


def next_x(value):
    return pltpu.roll(value, 112, 1)


def prev_x(value):
    return pltpu.roll(value, 16, 1)


def next_z(value):
    return pltpu.roll(value, 7, 0)


def prev_z(value):
    return pltpu.roll(value, 1, 0)


def total_of(value):
    for shift in (1, 2, 4):
        value = value + pltpu.roll(value, shift, 0)
    for shift in (8, 16, 32, 64):
        value = value + pltpu.roll(value, shift, 1)
    return value


SPOTS = [(xc, zc) for xc in range(XC) for zc in range(ZC)]


def plane(ref, yc, lead=()):
    return {(xc, zc): ref[(*lead, xc, yc, zc)] for xc, zc in SPOTS}


def ahead_x(values, xc, zc):
    return values[xc + 1, zc] if xc < XC - 1 else next_x(values[0, zc])


def back_x(values, xc, zc):
    return values[xc - 1, zc] if xc > 0 else prev_x(values[XC - 1, zc])


def ahead_z(values, xc, zc):
    return values[xc, zc + 1] if zc < ZC - 1 else next_z(values[xc, 0])


def back_z(values, xc, zc):
    return values[xc, zc - 1] if zc > 0 else prev_z(values[xc, ZC - 1])


def swapped(values):
    return {spot: swap_half(value) for spot, value in values.items()}


class Sum:
    def __init__(self, ways=4):
        self.parts = [None] * ways
        self.at = 0

    def add(self, value):
        slot = self.at % len(self.parts)
        self.at += 1
        self.parts[slot] = value if self.parts[slot] is None else self.parts[slot] + value

    def get(self):
        parts = [part for part in self.parts if part is not None]
        while len(parts) > 1:
            parts = [sum(parts[i : i + 2][1:], parts[i]) for i in range(0, len(parts), 2)]
        return parts[0]


def micro_kernel(
    phases_ref, grain_ref, pc_ref, counts_ref, current_ref, load_ref, states_ref, tangent_ref, mine_ref,
    rows, turned, cond, faces, rhs, fluct, remain, direction, image, scal,
):
    pc = [pc_ref[k] for k in range(PHASES)]
    for e in range(ELEMENTS):
        phase = phases_ref[0, 0, e]
        value = jnp.where(phase == 0, pc[0], jnp.where(phase == 1, pc[1], pc[2])) * grain_ref[0, 0, e]
        for yh in range(2):
            base = (yh * ELEMENTS + e) * VOX
            for t, (start, size) in enumerate(SPANS):
                rows[t, base : base + VOX, 0:size] = value[:, yh * HALF + start : yh * HALF + start + size]
    for xc in range(XC):
        for t, (start, size) in enumerate(SPANS):
            parts = []
            for xs in range(8):
                for yh in range(2):
                    parts.append(rows.at[t][pl.ds(yh * ELEMENTS * VOX + 3 * xs + xc, 8, stride=VOX), :])
            block = jnp.concatenate(parts, axis=0).T
            turned[xc * HALF + start : xc * HALF + start + size, :] = block[0:size]
    for xc in range(XC):
        for yc in range(YC):
            for zc in range(ZC):
                cond[xc, yc, zc] = turned[pl.ds(xc * HALF + yc * VOX + zc, 8, stride=3), :]

    face_sums = [Sum(), Sum(), Sum()]
    here = plane(cond, 0)
    for yc in range(YC):
        ahead = plane(cond, yc + 1) if yc < YC - 1 else swapped(plane(cond, 0))
        for xc, zc in SPOTS:
            own = here[xc, zc]
            for d, other in enumerate((ahead_x(here, xc, zc), ahead[xc, zc], ahead_z(here, xc, zc))):
                face = (own + other) * 0.5
                faces[d, xc, yc, zc] = face
                face_sums[d].add(face)
        here = ahead
    norms = [Sum(), Sum(), Sum()]
    before = swapped(plane(faces, YC - 1, (1,)))
    for yc in range(YC):
        fx, fy, fz = (plane(faces, yc, (d,)) for d in range(3))
        for xc, zc in SPOTS:
            backs = (back_x(fx, xc, zc), before[xc, zc], back_z(fz, xc, zc))
            for d, own in enumerate((fx[xc, zc], fy[xc, zc], fz[xc, zc])):
                value = own - backs[d]
                rhs[d, xc, yc, zc] = value
                remain[d, xc, yc, zc] = value
                norms[d].add(value * value)
        before = fy

    lane = lax.broadcasted_iota(jnp.int32, (8, 128), 1)
    counts = jnp.zeros((8, 128), jnp.int32)
    longest = counts_ref[0, 0, 0]
    for e in range(ELEMENTS):
        counts = jnp.where((lane & 7) == e, counts_ref[0, 0, e], counts)
        longest = jnp.maximum(longest, counts_ref[0, 0, e])

    def sweep(c, alpha, beta, first):
        curv = Sum()

        def fresh(yc):
            out = {}
            for xc, zc in SPOTS:
                at = (c, xc, yc, zc)
                if first:
                    value = remain[at]
                    fluct[at] = jnp.zeros((8, 128), jnp.float32)
                else:
                    old = direction[at]
                    fluct[at] = fluct[at] + alpha * old
                    value = remain[at] + beta * old
                direction[at] = value
                out[xc, zc] = value
            return out

        last = fresh(YC - 1)
        here = fresh(0)
        flow_back = {
            s: swap_half(faces[1, s[0], YC - 1, s[1]] * (last[s] - swap_half(here[s]))) for s in SPOTS
        }
        for yc in range(YC):
            if yc < YC - 2:
                ahead = fresh(yc + 1)
            elif yc == YC - 2:
                ahead = plane(direction, YC - 1, (c,))
            else:
                ahead = swapped(plane(direction, 0, (c,)))
            gx, gy, gz = {}, {}, {}
            for xc, zc in SPOTS:
                own = here[xc, zc]
                gx[xc, zc] = faces[0, xc, yc, zc] * (own - ahead_x(here, xc, zc))
                gy[xc, zc] = faces[1, xc, yc, zc] * (own - ahead[xc, zc])
                gz[xc, zc] = faces[2, xc, yc, zc] * (own - ahead_z(here, xc, zc))
            for xc, zc in SPOTS:
                value = (
                    (gx[xc, zc] - back_x(gx, xc, zc))
                    + (gy[xc, zc] - flow_back[xc, zc])
                    + (gz[xc, zc] - back_z(gz, xc, zc))
                )
                image[c, xc, yc, zc] = value
                curv.add(here[xc, zc] * value)
            flow_back = gy
            here = ahead
        return total_of(curv.get())

    def reduce_residual(c, alpha):
        norm = Sum()
        for yc in range(YC):
            for xc, zc in SPOTS:
                at = (c, xc, yc, zc)
                value = remain[at] - alpha * image[at]
                remain[at] = value
                norm.add(value * value)
        return total_of(norm.get())

    for c in range(3):
        norm = total_of(norms[c].get())
        curv = sweep(c, None, None, True)
        scal[0, c] = norm
        scal[1, c] = norm / curv

    def iterate(index, carry):
        for c in range(3):
            alpha = scal[1, c]
            norm = scal[0, c]
            norm_next = reduce_residual(c, alpha)
            curv = sweep(c, alpha, norm_next / norm, False)
            scal[0, c] = norm_next
            scal[1, c] = jnp.where(index < counts, norm_next / curv, 0.0)
        return carry

    lax.fori_loop(1, longest, iterate, 0)

    scale = 1.0 / (VOX * YZ)
    entries = {}
    for c in range(3):
        alpha = scal[1, c]
        sums = [Sum(2), Sum(2), Sum(2)]
        for xc in range(XC):
            for yc in range(YC):
                for zc in range(ZC):
                    at = (c, xc, yc, zc)
                    value = fluct[at] + alpha * direction[at]
                    turned[pl.ds(xc * HALF + yc * VOX + zc, 8, stride=3), :] = value
                    for d in range(3):
                        sums[d].add(value * rhs[d, xc, yc, zc])
        for d in range(3):
            entry = -sums[d].get()
            if d == c:
                entry = entry + face_sums[d].get()
            entries[d, c] = total_of(entry) * scale
        for xc in range(XC):
            for t, (start, size) in enumerate(SPANS):
                block = turned[xc * HALF + start : xc * HALF + start + size, :].T
                for xs in range(8):
                    for yh in range(2):
                        row = (xs * 2 + yh) * 8
                        piece = block[row : row + 8]
                        if size < 128:
                            piece = jnp.concatenate([piece, jnp.zeros((8, 128 - size), jnp.float32)], axis=1)
                        rows.at[t][pl.ds(yh * ELEMENTS * VOX + 3 * xs + xc, 8, stride=VOX), :] = piece
        for e in range(ELEMENTS):
            for yh in range(2):
                base = (yh * ELEMENTS + e) * VOX
                for t, (start, size) in enumerate(SPANS):
                    states_ref[0, 0, e, c, :, yh * HALF + start : yh * HALF + start + size] = rows[
                        t, base : base + VOX, 0:size
                    ]


    for d in range(3):
        for c in range(3):
            tangent_ref[0, d, c] = entries[d, c][0:1, 0:ELEMENTS]
    mine = jnp.where(lane < 8, entries[0, 0], jnp.where(lane < 16, entries[1, 1], entries[2, 2]))
    for e in range(ELEMENTS):
        mine = jnp.where(lane == 3 * ELEMENTS + e, current_ref[0, 0, e], mine)
        mine = jnp.where(lane == 4 * ELEMENTS + e, load_ref[0, 0, e], mine)
    mine_ref[...] = mine[0:1]


def micro(phases, grain, phase_cond, counts, current, load):
    field = pltpu.VMEM((3, XC, YC, ZC, 8, 128), jnp.float32)
    vmem = pl.BlockSpec(memory_space=pltpu.VMEM)
    smem = pl.BlockSpec(memory_space=pltpu.SMEM)
    return pl.pallas_call(
        micro_kernel,
        out_shape=(
            jax.ShapeDtypeStruct((1, 1, ELEMENTS, 3, VOX, YZ), jnp.float32),
            jax.ShapeDtypeStruct((1, 3, 3, 1, ELEMENTS), jnp.float32),
            jax.ShapeDtypeStruct((1, 128), jnp.float32),
        ),
        in_specs=[vmem, vmem, smem, smem, smem, smem],
        out_specs=(vmem, vmem, vmem),
        scratch_shapes=[
            pltpu.VMEM((3, 2 * ELEMENTS * VOX, 128), jnp.float32),
            pltpu.VMEM((XC * HALF, 128), jnp.float32),
            pltpu.VMEM((XC, YC, ZC, 8, 128), jnp.float32),
            field, field, field, field, field, field,
            pltpu.VMEM((2, 3, 8, 128), jnp.float32),
        ],
        name="micro",
    )(phases, grain, phase_cond, counts, current, load)


def macro_kernel(nrow, ncol, depth, mine_ref, out_ref, got, picked, own_sem, send_sems, recv_sems):
    n = nrow * ncol
    me = lax.axis_index("row") * ncol + lax.axis_index("col")

    def peer(k):
        other = lax.rem(me + k, n)
        return {"row": other // ncol, "col": lax.rem(other, ncol)}

    barrier = pltpu.get_barrier_semaphore()

    def greet(k, carry):
        pl.semaphore_signal(barrier, inc=1, device_id=peer(k), device_id_type=pl.DeviceIdType.MESH)
        return carry

    lax.fori_loop(1, n, greet, 0)
    own = pltpu.make_async_copy(mine_ref, got.at[me], own_sem)
    own.start()
    pl.semaphore_wait(barrier, n - 1)

    def copy(k):
        return pltpu.make_async_remote_copy(
            src_ref=mine_ref,
            dst_ref=got.at[me],
            send_sem=send_sems.at[k],
            recv_sem=recv_sems.at[k],
            device_id=peer(k),
            device_id_type=pl.DeviceIdType.MESH,
        )

    def send(k, carry):
        copy(k).start()
        return carry

    def finish(k, carry):
        copy(k).wait()
        return carry

    lax.fori_loop(1, n, send, 0)
    own.wait()
    lax.fori_loop(1, n, finish, 0)

    table = got[...].reshape(n, 128)
    lane = lax.broadcasted_iota(jnp.int32, (n, 128), 1)
    device = lax.broadcasted_iota(jnp.int32, (n, 128), 0)
    inside = lane < depth

    def field(q):
        value = table if q == 0 else pltpu.roll(table, 128 - q * depth, 1)
        return jnp.where(inside, value, 0.0)

    row_at, col_at = device // ncol, lax.rem(device, ncol)
    steps = (
        (0, ncol, row_at < nrow - 1), (0, -ncol, row_at > 0),
        (0, 1, col_at < ncol - 1), (0, -1, col_at > 0),
        (1, 1, lane < depth - 1), (1, -1, lane > 0),
    )

    def shifted(value, axis, step):
        length = n if axis == 0 else 128
        return pltpu.roll(value, (-step) % length, axis)

    weights = []
    centre = jnp.zeros((n, 128), jnp.float32)
    for index, (axis, step, has) in enumerate(steps):
        k = field(index // 2)
        pair = 0.5 * (k + jnp.where(has, shifted(k, axis, step), 0.0))
        centre = centre + pair
        weights.append(jnp.where(has & inside, pair, 0.0))
    centre = jnp.where(inside, centre, 0.0)

    def apply(value):
        parts = [weight * shifted(value, axis, step) for weight, (axis, step, _) in zip(weights, steps)]
        return centre * value - ((parts[0] + parts[1]) + (parts[2] + parts[3]) + (parts[4] + parts[5]))

    def total(value):
        value = jnp.sum(value.reshape(n // 8, 8, 128), axis=0)
        for shift in (1, 2, 4):
            value = value + pltpu.roll(value, shift, 0)
        return jnp.sum(value, axis=1, keepdims=True)[0:1]

    residual = field(4) - apply(field(3))
    increment = jnp.zeros((n, 128), jnp.float32)
    direction = residual
    norm = total(residual * residual)
    for _ in range(MACRO_ITERS):
        image = apply(direction)
        step_size = norm / total(direction * image)
        increment = increment + step_size * direction
        residual = residual - step_size * image
        norm_next = total(residual * residual)
        direction = residual + (norm_next / norm) * direction
        norm = norm_next
    picked[0] = increment
    picked[1] = residual
    out_ref[0:1] = picked[0, pl.ds(me, 1), :]
    out_ref[1:2] = picked[1, pl.ds(me, 1), :]


def part_kernel(both_ref, inc_ref, res_ref):
    depth = inc_ref.shape[2]
    inc_ref[0] = both_ref[0:1, 0:depth]
    res_ref[0] = both_ref[1:2, 0:depth]


def macro(mine, nrow, ncol, depth):
    n = nrow * ncol
    vmem = pl.BlockSpec(memory_space=pltpu.VMEM)
    small = jax.ShapeDtypeStruct((1, 1, depth), jnp.float32)
    both = pl.pallas_call(
        functools.partial(macro_kernel, nrow, ncol, depth),
        out_shape=jax.ShapeDtypeStruct((2, 128), jnp.float32),
        in_specs=[vmem],
        out_specs=vmem,
        scratch_shapes=[
            pltpu.VMEM((n, 1, 128), jnp.float32),
            pltpu.VMEM((2, n, 128), jnp.float32),
            pltpu.SemaphoreType.DMA,
            pltpu.SemaphoreType.DMA((n,)),
            pltpu.SemaphoreType.DMA((n,)),
        ],
        compiler_params=pltpu.CompilerParams(collective_id=0, has_side_effects=True),
        name="macro",
    )(mine)
    return pl.pallas_call(
        part_kernel, out_shape=(small, small), in_specs=[vmem], out_specs=(vmem, vmem), name="part"
    )(both)


def shards(nrow, ncol, phases, grain, phase_cond, micro_counts, current, load):
    depth = phases.shape[2]
    states, tangent, mine = micro(phases, grain, phase_cond, micro_counts, current, load)
    increment, residual = macro(mine, nrow, ncol, depth)
    return (states, tangent.transpose(0, 3, 4, 1, 2), increment, residual)


def solution(mesh):
    placed = (
        P("row", "col", None, None, None),
        P("row", "col", None, None, None),
        P(),
        P("row", "col", None),
        P("row", "col", None),
        P("row", "col", None),
    )
    return jax.shard_map(
        functools.partial(shards, mesh.shape["row"], mesh.shape["col"]),
        mesh=mesh,
        in_specs=placed,
        out_specs=(
            P("row", "col", None, None, None, None),
            P("row", "col", None, None, None),
            P("row", "col", None),
            P("row", "col", None),
        ),
        check_vma=False,
    )
```

profile of v0, /device:TPU:1, one launch (start us, length us, event | category | flops | bytes accessed | tf_op | source)
XLA Modules:
  0.0 61.2 jit_solution(13520896314632545727)
XLA Ops:
  0.6 26.0 %micro.1 = (f32[1,1,8,3,24,576]{5,4,3,2,1,0:T(8,128)}, f32[1,3,3,1,8]{4,3,2,1,0:T(1,128)}, f32[1,128]{1,0:T(1,128)}) custom-call(s32[1,1,8,24,576]{4,3,2,1,0:T(8,128)} %phases_ref.1, f32[1,1,8,24,576]{4,3,2,1,0:T(8,128)} %grain_ref.1, f32[3]{0:T(128)} %pc_ref.1, s32[1,1,8]{2,1,0:T(1,128)} %counts_ref.1, f32[1,1,8]{2,1,0:T(1,128)} %current_ref.1, ...), custom_call_target="tpu_custom_call" | custom-call | tf_op jit(solution)/shard_map/micro/pallas_call | solution.py:277
  26.7 33.3 %macro.1.both_ref = f32[2,128]{1,0:T(2,128)} custom-call(f32[1,128]{1,0:T(1,128)} %get-tuple-element.11.mine_ref), custom_call_target="tpu_custom_call" | custom-call | tf_op jit(solution)/shard_map/macro/pallas_call | solution.py:405
  60.0 1.2 %part.1 = (f32[1,1,8]{2,1,0:T(1,128)}, f32[1,1,8]{2,1,0:T(1,128)}) custom-call(f32[2,128]{1,0:T(2,128)} %macro.1.both_ref), custom_call_target="tpu_custom_call" | custom-call | tf_op jit(solution)/shard_map/part/pallas_call | solution.py:420
where the time goes:
time: 61.7 us; the launch traced here: 61.2 us
  Pallas kernels  60.5 us (98%)
  between operations  0.64 us (1%)
    pallas_call x1, Pallas kernels, macro(): pl.pallas_call(functools.partial(macro_kernel, nrow, ncol, depth), out_sh...  33.3 us
    pallas_call x1, Pallas kernels, micro(): pl.pallas_call(micro_kernel, out_shape=(jax.ShapeDtypeStruct((1, 1, ELEME...  26 us

commit v1 on v0

--- a/solution.py
+++ b/solution.py
@@ -11,6 +11,7 @@
 YZ = 576
 PHASES = 3
 MACRO_ITERS = 8
+MICRO_MAX = 12
 
 XC, YC, ZC = 3, 12, 3
 ELEMENTS = 8
@@ -91,10 +92,44 @@
         return parts[0]
 
 
-def micro_kernel(
-    phases_ref, grain_ref, pc_ref, counts_ref, current_ref, load_ref, states_ref, tangent_ref, mine_ref,
-    rows, turned, cond, faces, rhs, fluct, remain, direction, image, scal,
+def far_first(nrow, ncol):
+    ny, nx = nrow // 2, 4
+    nz = ncol // nx
+    offsets = [
+        (y, core, x, z) for y in range(ny) for core in range(2) for x in range(nx) for z in range(nz)
+    ]
+
+    def hops(offset):
+        y, core, x, z = offset
+        return min(y, ny - y) + min(x, nx - x) + min(z, nz - z) + 0.5 * core
+
+    return sorted(offsets[1:], key=hops, reverse=True)
+
+
+def peer_of(row, col, offset, nrow, ncol):
+    ny, nx = nrow // 2, 4
+    nz = ncol // nx
+    y, core, x, z = offset
+    return {
+        "row": lax.rem(row // 2 + y, ny) * 2 + lax.rem(row + core, 2),
+        "col": lax.rem(col // nz + x, nx) * nz + lax.rem(lax.rem(col, nz) + z, nz),
+    }
+
+
+def fused_kernel(
+    nrow, ncol,
+    phases_ref, grain_ref, pc_ref, counts_ref, current_ref, load_ref, states_ref, tangent_ref, table_ref,
+    rows, turned, cond, faces, rhs, fluct, remain, direction, image, scal, mine, got, own_sem, send_sem, recv_sem,
 ):
+    n = nrow * ncol
+    row, col = lax.axis_index("row"), lax.axis_index("col")
+    offsets = far_first(nrow, ncol)
+    barrier = pltpu.get_barrier_semaphore()
+    for offset in offsets:
+        pl.semaphore_signal(
+            barrier, inc=1, device_id=peer_of(row, col, offset, nrow, ncol), device_id_type=pl.DeviceIdType.MESH
+        )
+
     pc = [pc_ref[k] for k in range(PHASES)]
     for e in range(ELEMENTS):
         phase = phases_ref[0, 0, e]
@@ -142,10 +177,11 @@
 
     lane = lax.broadcasted_iota(jnp.int32, (8, 128), 1)
     counts = jnp.zeros((8, 128), jnp.int32)
-    longest = counts_ref[0, 0, 0]
+    coarse = [jnp.zeros((8, 128), jnp.float32)] * 2
     for e in range(ELEMENTS):
-        counts = jnp.where((lane & 7) == e, counts_ref[0, 0, e], counts)
-        longest = jnp.maximum(longest, counts_ref[0, 0, e])
+        here_e = (lane & 7) == e
+        counts = jnp.where(here_e, counts_ref[0, 0, e], counts)
+        coarse = [jnp.where(here_e, ref[0, 0, e], value) for ref, value in zip((current_ref, load_ref), coarse)]
 
     def sweep(c, alpha, beta, first):
         curv = Sum()
@@ -209,21 +245,47 @@
         norm = total_of(norms[c].get())
         curv = sweep(c, None, None, True)
         scal[0, c] = norm
-        scal[1, c] = norm / curv
+        alpha = norm / curv
+        scal[1, c] = alpha
+        scal[2, c] = alpha * norm
 
     def iterate(index, carry):
         for c in range(3):
             alpha = scal[1, c]
             norm = scal[0, c]
             norm_next = reduce_residual(c, alpha)
-            curv = sweep(c, alpha, norm_next / norm, False)
+            active = index < counts
+            curv = sweep(c, alpha, jnp.where(active, norm_next / norm, 0.0), False)
             scal[0, c] = norm_next
-            scal[1, c] = jnp.where(index < counts, norm_next / curv, 0.0)
+            alpha = jnp.where(active, norm_next / curv, 0.0)
+            scal[1, c] = alpha
+            scal[2, c] = scal[2, c] + alpha * norm_next
         return carry
 
-    lax.fori_loop(1, longest, iterate, 0)
+    lax.fori_loop(1, MICRO_MAX, iterate, 0)
 
     scale = 1.0 / (VOX * YZ)
+    face_totals = [total_of(part.get()) for part in face_sums]
+    fields = [(face_totals[d] - scal[2, d]) * scale for d in range(3)] + coarse
+    slot = ((lane >> 3) - col) & 15
+    packed = fields[4]
+    for f in range(4):
+        packed = jnp.where(slot == f, fields[f], packed)
+    mine[...] = packed[0:1]
+
+    me = col * nrow + row
+    pl.semaphore_wait(barrier, n - 1)
+    got[pl.ds(me, 1)] = packed[0:1]
+    for offset in offsets:
+        pltpu.make_async_remote_copy(
+            src_ref=mine,
+            dst_ref=got.at[pl.ds(me, 1)],
+            send_sem=send_sem,
+            recv_sem=recv_sem,
+            device_id=peer_of(row, col, offset, nrow, ncol),
+            device_id_type=pl.DeviceIdType.MESH,
+        ).start()
+
     entries = {}
     for c in range(3):
         alpha = scal[1, c]
@@ -237,10 +299,8 @@
                     for d in range(3):
                         sums[d].add(value * rhs[d, xc, yc, zc])
         for d in range(3):
-            entry = -sums[d].get()
-            if d == c:
-                entry = entry + face_sums[d].get()
-            entries[d, c] = total_of(entry) * scale
+            entry = total_of(sums[d].get())
+            entries[d, c] = ((face_totals[d] - entry) if d == c else -entry) * scale
         for xc in range(XC):
             for t, (start, size) in enumerate(SPANS):
                 block = turned[xc * HALF + start : xc * HALF + start + size, :].T
@@ -263,23 +323,38 @@
     for d in range(3):
         for c in range(3):
             tangent_ref[0, d, c] = entries[d, c][0:1, 0:ELEMENTS]
-    mine = jnp.where(lane < 8, entries[0, 0], jnp.where(lane < 16, entries[1, 1], entries[2, 2]))
-    for e in range(ELEMENTS):
-        mine = jnp.where(lane == 3 * ELEMENTS + e, current_ref[0, 0, e], mine)
-        mine = jnp.where(lane == 4 * ELEMENTS + e, load_ref[0, 0, e], mine)
-    mine_ref[...] = mine[0:1]
-
-
-def micro(phases, grain, phase_cond, counts, current, load):
+
+    whole = pltpu.make_async_remote_copy(
+        src_ref=got.at[pl.ds(0, n - 1)],
+        dst_ref=got.at[pl.ds(0, n - 1)],
+        send_sem=send_sem,
+        recv_sem=recv_sem,
+        device_id=peer_of(row, col, offsets[0], nrow, ncol),
+        device_id_type=pl.DeviceIdType.MESH,
+    )
+    whole.wait_recv()
+    group = lane >> 3
+    for half in range(2):
+        found = [jnp.zeros((8, 128), jnp.float32)] * 5
+        for c in range(ncol // 2):
+            block = got[8 * (half * (ncol // 2) + c) : 8 * (half * (ncol // 2) + c) + 8]
+            for f in range(5):
+                found[f] = jnp.where(group == (c + f) % 16, block, found[f])
+        for f in range(5):
+            table_ref[f, half] = found[f]
+    whole.wait_send()
+
+
+def fused(phases, grain, phase_cond, counts, current, load, nrow, ncol):
     field = pltpu.VMEM((3, XC, YC, ZC, 8, 128), jnp.float32)
     vmem = pl.BlockSpec(memory_space=pltpu.VMEM)
     smem = pl.BlockSpec(memory_space=pltpu.SMEM)
     return pl.pallas_call(
-        micro_kernel,
+        functools.partial(fused_kernel, nrow, ncol),
         out_shape=(
             jax.ShapeDtypeStruct((1, 1, ELEMENTS, 3, VOX, YZ), jnp.float32),
             jax.ShapeDtypeStruct((1, 3, 3, 1, ELEMENTS), jnp.float32),
-            jax.ShapeDtypeStruct((1, 128), jnp.float32),
+            jax.ShapeDtypeStruct((5, 2, 8, 128), jnp.float32),
         ),
         in_specs=[vmem, vmem, smem, smem, smem, smem],
         out_specs=(vmem, vmem, vmem),
@@ -288,144 +363,141 @@
             pltpu.VMEM((XC * HALF, 128), jnp.float32),
             pltpu.VMEM((XC, YC, ZC, 8, 128), jnp.float32),
             field, field, field, field, field, field,
-            pltpu.VMEM((2, 3, 8, 128), jnp.float32),
+            pltpu.VMEM((3, 3, 8, 128), jnp.float32),
+            pltpu.VMEM((1, 128), jnp.float32),
+            pltpu.VMEM((nrow * ncol, 128), jnp.float32),
+            pltpu.SemaphoreType.DMA,
+            pltpu.SemaphoreType.DMA,
+            pltpu.SemaphoreType.DMA,
         ],
-        name="micro",
+        compiler_params=pltpu.CompilerParams(collective_id=0, has_side_effects=True, vmem_limit_bytes=40 * 2**20),
+        name="fused",
     )(phases, grain, phase_cond, counts, current, load)
 
 
-def macro_kernel(nrow, ncol, depth, mine_ref, out_ref, got, picked, own_sem, send_sems, recv_sems):
-    n = nrow * ncol
-    me = lax.axis_index("row") * ncol + lax.axis_index("col")
-
-    def peer(k):
-        other = lax.rem(me + k, n)
-        return {"row": other // ncol, "col": lax.rem(other, ncol)}
-
-    barrier = pltpu.get_barrier_semaphore()
-
-    def greet(k, carry):
-        pl.semaphore_signal(barrier, inc=1, device_id=peer(k), device_id_type=pl.DeviceIdType.MESH)
-        return carry
-
-    lax.fori_loop(1, n, greet, 0)
-    own = pltpu.make_async_copy(mine_ref, got.at[me], own_sem)
-    own.start()
-    pl.semaphore_wait(barrier, n - 1)
-
-    def copy(k):
-        return pltpu.make_async_remote_copy(
-            src_ref=mine_ref,
-            dst_ref=got.at[me],
-            send_sem=send_sems.at[k],
-            recv_sem=recv_sems.at[k],
-            device_id=peer(k),
-            device_id_type=pl.DeviceIdType.MESH,
-        )
-
-    def send(k, carry):
-        copy(k).start()
-        return carry
-
-    def finish(k, carry):
-        copy(k).wait()
-        return carry
-
-    lax.fori_loop(1, n, send, 0)
-    own.wait()
-    lax.fori_loop(1, n, finish, 0)
-
-    table = got[...].reshape(n, 128)
-    lane = lax.broadcasted_iota(jnp.int32, (n, 128), 1)
-    device = lax.broadcasted_iota(jnp.int32, (n, 128), 0)
-    inside = lane < depth
-
-    def field(q):
-        value = table if q == 0 else pltpu.roll(table, 128 - q * depth, 1)
-        return jnp.where(inside, value, 0.0)
-
-    row_at, col_at = device // ncol, lax.rem(device, ncol)
-    steps = (
-        (0, ncol, row_at < nrow - 1), (0, -ncol, row_at > 0),
-        (0, 1, col_at < ncol - 1), (0, -1, col_at > 0),
-        (1, 1, lane < depth - 1), (1, -1, lane > 0),
+def coarse_kernel(ncol, table_ref, tangent_in, states_in, inc_ref, res_ref, tangent_ref, states_ref, out_sems):
+    stores = [pltpu.make_async_copy(states_in.at[0, 0, e], states_ref.at[0, 0, e], out_sems.at[e]) for e in range(ELEMENTS)]
+    for copy in stores:
+        copy.start()
+    tangent_ref[...] = tangent_in[...]
+
+    lane = lax.broadcasted_iota(jnp.int32, (8, 128), 1)
+    ex = lax.broadcasted_iota(jnp.int32, (8, 128), 0)
+    group, ez = lane >> 3, lane & 7
+
+    def field(f):
+        return [pltpu.roll(table_ref[f, h], (128 - 8 * f) % 128, 1) for h in range(2)]
+
+    def x_up(v):
+        return [pltpu.roll(part, 7, 0) for part in v]
+
+    def x_down(v):
+        return [pltpu.roll(part, 1, 0) for part in v]
+
+    def y_up(v):
+        first, second = (pltpu.roll(part, 120, 1) for part in v)
+        return [jnp.where(group < 15, first, second), second]
+
+    def y_down(v):
+        first, second = (pltpu.roll(part, 8, 1) for part in v)
+        return [first, jnp.where(group > 0, second, first)]
+
+    def z_up(v):
+        return [pltpu.roll(part, 127, 1) for part in v]
+
+    def z_down(v):
+        return [pltpu.roll(part, 1, 1) for part in v]
+
+    yes = ex >= 0
+    moves = (
+        (0, x_up, [ex < 7] * 2), (0, x_down, [ex > 0] * 2),
+        (1, y_up, [yes, group < 15]), (1, y_down, [group > 0, yes]),
+        (2, z_up, [ez < 7] * 2), (2, z_down, [ez > 0] * 2),
     )
-
-    def shifted(value, axis, step):
-        length = n if axis == 0 else 128
-        return pltpu.roll(value, (-step) % length, axis)
-
+    centre = [jnp.zeros((8, 128), jnp.float32)] * 2
     weights = []
-    centre = jnp.zeros((n, 128), jnp.float32)
-    for index, (axis, step, has) in enumerate(steps):
-        k = field(index // 2)
-        pair = 0.5 * (k + jnp.where(has, shifted(k, axis, step), 0.0))
-        centre = centre + pair
-        weights.append(jnp.where(has & inside, pair, 0.0))
-    centre = jnp.where(inside, centre, 0.0)
-
-    def apply(value):
-        parts = [weight * shifted(value, axis, step) for weight, (axis, step, _) in zip(weights, steps)]
-        return centre * value - ((parts[0] + parts[1]) + (parts[2] + parts[3]) + (parts[4] + parts[5]))
-
-    def total(value):
-        value = jnp.sum(value.reshape(n // 8, 8, 128), axis=0)
+    kd = [field(d) for d in range(3)]
+    for d, move, has in moves:
+        other = move(kd[d])
+        pair = [0.5 * (own + jnp.where(ok, far, 0.0)) for own, far, ok in zip(kd[d], other, has)]
+        centre = [c + p for c, p in zip(centre, pair)]
+        weights.append([jnp.where(ok, p, 0.0) for p, ok in zip(pair, has)])
+
+    def apply(v):
+        moved = [move(v) for _, move, _ in moves]
+        out = []
+        for h in range(2):
+            parts = [weights[i][h] * moved[i][h] for i in range(6)]
+            out.append(centre[h] * v[h] - ((parts[0] + parts[1]) + (parts[2] + parts[3]) + (parts[4] + parts[5])))
+        return out
+
+    def total(u, v):
+        value = u[0] * v[0] + u[1] * v[1]
         for shift in (1, 2, 4):
             value = value + pltpu.roll(value, shift, 0)
-        return jnp.sum(value, axis=1, keepdims=True)[0:1]
-
-    residual = field(4) - apply(field(3))
-    increment = jnp.zeros((n, 128), jnp.float32)
-    direction = residual
-    norm = total(residual * residual)
-    for _ in range(MACRO_ITERS):
-        image = apply(direction)
-        step_size = norm / total(direction * image)
-        increment = increment + step_size * direction
-        residual = residual - step_size * image
-        norm_next = total(residual * residual)
-        direction = residual + (norm_next / norm) * direction
-        norm = norm_next
-    picked[0] = increment
-    picked[1] = residual
-    out_ref[0:1] = picked[0, pl.ds(me, 1), :]
-    out_ref[1:2] = picked[1, pl.ds(me, 1), :]
-
-
-def part_kernel(both_ref, inc_ref, res_ref):
-    depth = inc_ref.shape[2]
-    inc_ref[0] = both_ref[0:1, 0:depth]
-    res_ref[0] = both_ref[1:2, 0:depth]
-
-
-def macro(mine, nrow, ncol, depth):
-    n = nrow * ncol
+        return jnp.sum(value, axis=1, keepdims=True)
+
+    def axpy(a, u, v):
+        return [a * p + q for p, q in zip(u, v)]
+
+    image = apply(field(3))
+    residual = [p - q for p, q in zip(field(4), image)]
+    image = apply(residual)
+    increment = older = alpha = None
+    for i in range(MACRO_ITERS):
+        gamma, delta = total(residual, residual), total(image, residual)
+        deep = apply(image) if i < MACRO_ITERS - 1 else None
+        if i == 0:
+            alpha = gamma / delta
+            p, s, z = residual, image, deep
+            increment = [alpha * v for v in p]
+        else:
+            beta = gamma / older
+            alpha = gamma / (delta - beta * gamma / alpha)
+            p, s = axpy(beta, p, residual), axpy(beta, s, image)
+            z = axpy(beta, z, deep) if deep is not None else None
+            increment = axpy(alpha, p, increment)
+        older = gamma
+        residual = axpy(-alpha, s, residual)
+        if deep is not None:
+            image = axpy(-alpha, z, image)
+
+    row, col = lax.axis_index("row"), lax.axis_index("col")
+    for value, ref in ((increment, inc_ref), (residual, res_ref)):
+        own = jnp.where(ex == row, jnp.where(col < 16, value[0], value[1]), 0.0)
+        own = jnp.where(group == (col & 15), own, 0.0)
+        for shift in (1, 2, 4):
+            own = own + pltpu.roll(own, shift, 0)
+        own = pltpu.roll(own, (128 - 8 * (col & 15)) & 127, 1)
+        ref[0] = own[0:1, 0:ELEMENTS]
+    for outgoing in stores:
+        outgoing.wait()
+
+
+def coarse(table, tangent, states, ncol):
     vmem = pl.BlockSpec(memory_space=pltpu.VMEM)
-    small = jax.ShapeDtypeStruct((1, 1, depth), jnp.float32)
-    both = pl.pallas_call(
-        functools.partial(macro_kernel, nrow, ncol, depth),
-        out_shape=jax.ShapeDtypeStruct((2, 128), jnp.float32),
-        in_specs=[vmem],
-        out_specs=vmem,
+    anywhere = pl.BlockSpec(memory_space=pl.ANY)
+    small = jax.ShapeDtypeStruct((1, 1, ELEMENTS), jnp.float32)
+    return pl.pallas_call(
+        functools.partial(coarse_kernel, ncol),
+        out_shape=(
+            small, small,
+            jax.ShapeDtypeStruct(tangent.shape, jnp.float32),
+            jax.ShapeDtypeStruct(states.shape, jnp.float32),
+        ),
+        in_specs=[vmem, vmem, anywhere],
+        out_specs=(vmem, vmem, vmem, anywhere),
         scratch_shapes=[
-            pltpu.VMEM((n, 1, 128), jnp.float32),
-            pltpu.VMEM((2, n, 128), jnp.float32),
-            pltpu.SemaphoreType.DMA,
-            pltpu.SemaphoreType.DMA((n,)),
-            pltpu.SemaphoreType.DMA((n,)),
+            pltpu.SemaphoreType.DMA((ELEMENTS,)),
         ],
-        compiler_params=pltpu.CompilerParams(collective_id=0, has_side_effects=True),
-        name="macro",
-    )(mine)
-    return pl.pallas_call(
-        part_kernel, out_shape=(small, small), in_specs=[vmem], out_specs=(vmem, vmem), name="part"
-    )(both)
+        compiler_params=pltpu.CompilerParams(vmem_limit_bytes=16 * 2**20),
+        name="coarse",
+    )(table, tangent, states)
 
 
 def shards(nrow, ncol, phases, grain, phase_cond, micro_counts, current, load):
-    depth = phases.shape[2]
-    states, tangent, mine = micro(phases, grain, phase_cond, micro_counts, current, load)
-    increment, residual = macro(mine, nrow, ncol, depth)
+    states, tangent, table = fused(phases, grain, phase_cond, micro_counts, current, load, nrow, ncol)
+    increment, residual, tangent, states = coarse(table, tangent, states, ncol)
     return (states, tangent.transpose(0, 3, 4, 1, 2), increment, residual)
 
 

time: 61.7 us -> 47.7 us (0.77)
  Pallas kernels: 60.5 us -> 42.1 us
  local copies, waits for them, and re-layouts: 0 us -> 4.67 us
    pallas_call x3 -> x2, Pallas kernels: 60.5 us -> 42.1 us  [the longest x1 39.5 us: fused(): pl.pallas_call(functools.partial(fused_kernel, nrow, ncol), out_shape=(ja...]
    unnamed x0 -> x12, local copies, waits for them, and re-layouts: none -> 4.67 us
where the time goes in v1:
time: 47.7 us; the launch traced here: 47.5 us
  Pallas kernels  42.1 us (88%)
  local copies, waits for them, and re-layouts  4.67 us (10%)
  between operations  0.65 us (1%)
    pallas_call x1, Pallas kernels, fused(): pl.pallas_call(functools.partial(fused_kernel, nrow, ncol), out_shape=(ja...  39.5 us
    unnamed x12, local copies, waits for them, and re-layouts  4.67 us
    pallas_call x1, Pallas kernels, coarse(): pl.pallas_call(functools.partial(coarse_kernel, ncol), out_shape=(small,...  2.66 us

profile of v1, /device:TPU:1, one launch (start us, length us, event | category | flops | bytes accessed | tf_op | source)
XLA Modules:
  0.0 47.5 jit_solution(10781453683403383759)
XLA Ops:
  0.6 0.0 copy-start
  0.6 1.0 %copy-done = s32[1,1,8,24,576]{4,3,2,1,0:T(8,128)S(1)} copy-done((s32[1,1,8,24,576]{4,3,2,1,0:T(8,128)S(1)}, s32[1,1,8,24,576]{4,3,2,1,0:T(8,128)}, u32[]{:S(2)}) %copy-start) | copy-done | bytes 442392
  1.7 0.0 copy-start.1
  1.7 1.0 %copy-done.1 = f32[1,1,8,24,576]{4,3,2,1,0:T(8,128)S(1)} copy-done((f32[1,1,8,24,576]{4,3,2,1,0:T(8,128)S(1)}, f32[1,1,8,24,576]{4,3,2,1,0:T(8,128)}, u32[]{:S(2)}) %copy-start.1) | copy-done | bytes 442392
  2.7 0.0 copy-start.2
  2.7 0.7 %copy-done.2 = f32[3]{0:T(128)S(1)} copy-done((f32[3]{0:T(128)S(1)}, f32[3]{0:T(128)}, u32[]{:S(2)}) %copy-start.2) | copy-done | bytes 36
  3.4 0.0 copy-start.3
  3.4 0.7 %copy-done.3 = s32[1,1,8]{2,1,0:T(1,128)S(1)} copy-done((s32[1,1,8]{2,1,0:T(1,128)S(1)}, s32[1,1,8]{2,1,0:T(1,128)}, u32[]{:S(2)}) %copy-start.3) | copy-done | bytes 56
  4.0 0.0 copy-start.4
  4.0 0.7 %copy-done.4 = f32[1,1,8]{2,1,0:T(1,128)S(1)} copy-done((f32[1,1,8]{2,1,0:T(1,128)S(1)}, f32[1,1,8]{2,1,0:T(1,128)}, u32[]{:S(2)}) %copy-start.4) | copy-done | bytes 56
  4.7 0.0 copy-start.5
  4.7 0.7 %copy-done.5 = f32[1,1,8]{2,1,0:T(1,128)S(1)} copy-done((f32[1,1,8]{2,1,0:T(1,128)S(1)}, f32[1,1,8]{2,1,0:T(1,128)}, u32[]{:S(2)}) %copy-start.5) | copy-done | bytes 56
  5.3 39.5 %fused.1 = (f32[1,1,8,3,24,576]{5,4,3,2,1,0:T(8,128)S(1)}, f32[1,3,3,1,8]{4,3,2,1,0:T(1,128)S(1)}, f32[5,2,8,128]{3,2,1,0:T(8,128)S(1)}) custom-call(s32[1,1,8,24,576]{4,3,2,1,0:T(8,128)S(1)} %copy-done, f32[1,1,8,24,576]{4,3,2,1,0:T(8,128)S(1)} %copy-done.1, f32[3]{0:T(128)S(1)} %copy-done.2, s32[1,1,8]{2,1,0:T(1,128)S(1)} %copy-done.3, ...), custom_call_target="tpu_custom_call" | custom-call | tf_op jit(solution)/shard_map/fused/pallas_call | solution.py:352
  44.8 2.7 %coarse.1 = (f32[1,1,8]{2,1,0:T(1,128)}, f32[1,1,8]{2,1,0:T(1,128)}, f32[1,3,3,1,8]{4,3,2,1,0:T(1,128)}, f32[1,1,8,3,24,576]{5,4,3,2,1,0:T(8,128)}) custom-call(f32[5,2,8,128]{3,2,1,0:T(8,128)S(1)} %get-tuple-element.11.table_ref, f32[1,3,3,1,8]{4,3,2,1,0:T(1,128)S(1)} %get-tuple-element.12.tangent_in, f32[1,1,8,3,24,576]{5,4,3,2,1,0:T(8,128)S(1)} %get-tuple-element.13.states_in), custom_call_target="tpu_custom_call" | custom-call | tf_op jit(solution)/shard_map/coarse/pallas_call | solution.py:481
Async XLA Ops:
  0.6 1.0 %copy-start = (s32[1,1,8,24,576]{4,3,2,1,0:T(8,128)S(1)}, s32[1,1,8,24,576]{4,3,2,1,0:T(8,128)}, u32[]{:S(2)}) copy-start(s32[1,1,8,24,576]{4,3,2,1,0:T(8,128)} %phases_ref.1) | copy-start | bytes 1327108
  1.7 1.0 %copy-start.1 = (f32[1,1,8,24,576]{4,3,2,1,0:T(8,128)S(1)}, f32[1,1,8,24,576]{4,3,2,1,0:T(8,128)}, u32[]{:S(2)}) copy-start(f32[1,1,8,24,576]{4,3,2,1,0:T(8,128)} %grain_ref.1) | copy-start | bytes 1327108
  2.7 0.7 %copy-start.2 = (f32[3]{0:T(128)S(1)}, f32[3]{0:T(128)}, u32[]{:S(2)}) copy-start(f32[3]{0:T(128)} %pc_ref.1) | copy-start | bytes 40
  3.4 0.7 %copy-start.3 = (s32[1,1,8]{2,1,0:T(1,128)S(1)}, s32[1,1,8]{2,1,0:T(1,128)}, u32[]{:S(2)}) copy-start(s32[1,1,8]{2,1,0:T(1,128)} %counts_ref.1) | copy-start | bytes 100
  4.0 0.7 %copy-start.4 = (f32[1,1,8]{2,1,0:T(1,128)S(1)}, f32[1,1,8]{2,1,0:T(1,128)}, u32[]{:S(2)}) copy-start(f32[1,1,8]{2,1,0:T(1,128)} %current_ref.1) | copy-start | bytes 100
  4.7 0.7 %copy-start.5 = (f32[1,1,8]{2,1,0:T(1,128)S(1)}, f32[1,1,8]{2,1,0:T(1,128)}, u32[]{:S(2)}) copy-start(f32[1,1,8]{2,1,0:T(1,128)} %load_ref.1) | copy-start | bytes 100

commit v2 on v1

--- a/solution.py
+++ b/solution.py
@@ -43,9 +43,10 @@
 def total_of(value):
     for shift in (1, 2, 4):
         value = value + pltpu.roll(value, shift, 0)
-    for shift in (8, 16, 32, 64):
-        value = value + pltpu.roll(value, shift, 1)
-    return value
+    k = lax.broadcasted_iota(jnp.int32, (128, 128), 0)
+    j = lax.broadcasted_iota(jnp.int32, (128, 128), 1)
+    same = jnp.where((k & 7) == (j & 7), 1.0, 0.0)
+    return jnp.dot(value, same, precision=lax.Precision.HIGHEST, preferred_element_type=jnp.float32)
 
 
 SPOTS = [(xc, zc) for xc in range(XC) for zc in range(ZC)]
@@ -59,7 +60,9 @@
     return values[xc + 1, zc] if xc < XC - 1 else next_x(values[0, zc])
 
 
-def back_x(values, xc, zc):
+def back_x(values, xc, zc, wrap=None):
+    if wrap is not None and xc == 0:
+        return wrap[zc]
     return values[xc - 1, zc] if xc > 0 else prev_x(values[XC - 1, zc])
 
 
@@ -118,11 +121,27 @@
 
 def fused_kernel(
     nrow, ncol,
-    phases_ref, grain_ref, pc_ref, counts_ref, current_ref, load_ref, states_ref, tangent_ref, table_ref,
-    rows, turned, cond, faces, rhs, fluct, remain, direction, image, scal, mine, got, own_sem, send_sem, recv_sem,
+    phases_in, grain_in, pc_in, counts_in, current_in, load_in, states_ref, tangent_ref, table_ref,
+    phases_ref, grain_ref, pc_ref, counts_ref, current_ref, load_ref, in_sems, back_faces, placed, out_sems,
+    rows, turned, cond, faces, rhs, fluct, remain, direction, image, scal, mine, got, send_sem, recv_sem,
 ):
     n = nrow * ncol
     row, col = lax.axis_index("row"), lax.axis_index("col")
+    smalls = [
+        pltpu.make_async_copy(source, target, in_sems.at[ELEMENTS + i])
+        for i, (source, target) in enumerate(
+            ((pc_in, pc_ref), (counts_in, counts_ref), (current_in, current_ref), (load_in, load_ref))
+        )
+    ]
+    voxels = [
+        [
+            pltpu.make_async_copy(source.at[0, 0, e], target.at[0, 0, e], in_sems.at[e])
+            for source, target in ((phases_in, phases_ref), (grain_in, grain_ref))
+        ]
+        for e in range(ELEMENTS)
+    ]
+    for copy in smalls + sum(voxels, []):
+        copy.start()
     offsets = far_first(nrow, ncol)
     barrier = pltpu.get_barrier_semaphore()
     for offset in offsets:
@@ -130,8 +149,12 @@
             barrier, inc=1, device_id=peer_of(row, col, offset, nrow, ncol), device_id_type=pl.DeviceIdType.MESH
         )
 
+    for copy in smalls:
+        copy.wait()
     pc = [pc_ref[k] for k in range(PHASES)]
     for e in range(ELEMENTS):
+        for copy in voxels[e]:
+            copy.wait()
         phase = phases_ref[0, 0, e]
         value = jnp.where(phase == 0, pc[0], jnp.where(phase == 1, pc[1], pc[2])) * grain_ref[0, 0, e]
         for yh in range(2):
@@ -171,6 +194,8 @@
             for d, own in enumerate((fx[xc, zc], fy[xc, zc], fz[xc, zc])):
                 value = own - backs[d]
                 rhs[d, xc, yc, zc] = value
+                if d == 0 and xc == 0:
+                    back_faces[yc, zc] = backs[0]
                 remain[d, xc, yc, zc] = value
                 norms[d].add(value * value)
         before = fy
@@ -219,9 +244,10 @@
                 gx[xc, zc] = faces[0, xc, yc, zc] * (own - ahead_x(here, xc, zc))
                 gy[xc, zc] = faces[1, xc, yc, zc] * (own - ahead[xc, zc])
                 gz[xc, zc] = faces[2, xc, yc, zc] * (own - ahead_z(here, xc, zc))
+            wrap = [back_faces[yc, zc] * (prev_x(here[XC - 1, zc]) - here[0, zc]) for zc in range(ZC)]
             for xc, zc in SPOTS:
                 value = (
-                    (gx[xc, zc] - back_x(gx, xc, zc))
+                    (gx[xc, zc] - back_x(gx, xc, zc, wrap))
                     + (gy[xc, zc] - flow_back[xc, zc])
                     + (gz[xc, zc] - back_z(gz, xc, zc))
                 )
@@ -315,7 +341,7 @@
             for yh in range(2):
                 base = (yh * ELEMENTS + e) * VOX
                 for t, (start, size) in enumerate(SPANS):
-                    states_ref[0, 0, e, c, :, yh * HALF + start : yh * HALF + start + size] = rows[
+                    placed[e, c, :, yh * HALF + start : yh * HALF + start + size] = rows[
                         t, base : base + VOX, 0:size
                     ]
 
@@ -323,6 +349,10 @@
     for d in range(3):
         for c in range(3):
             tangent_ref[0, d, c] = entries[d, c][0:1, 0:ELEMENTS]
+
+    stores = [pltpu.make_async_copy(placed.at[e], states_ref.at[0, 0, e], out_sems.at[e]) for e in range(ELEMENTS)]
+    for copy in stores:
+        copy.start()
 
     whole = pltpu.make_async_remote_copy(
         src_ref=got.at[pl.ds(0, n - 1)],
@@ -343,12 +373,13 @@
         for f in range(5):
             table_ref[f, half] = found[f]
     whole.wait_send()
+    for copy in stores:
+        copy.wait()
 
 
 def fused(phases, grain, phase_cond, counts, current, load, nrow, ncol):
     field = pltpu.VMEM((3, XC, YC, ZC, 8, 128), jnp.float32)
     vmem = pl.BlockSpec(memory_space=pltpu.VMEM)
-    smem = pl.BlockSpec(memory_space=pltpu.SMEM)
     return pl.pallas_call(
         functools.partial(fused_kernel, nrow, ncol),
         out_shape=(
@@ -356,9 +387,19 @@
             jax.ShapeDtypeStruct((1, 3, 3, 1, ELEMENTS), jnp.float32),
             jax.ShapeDtypeStruct((5, 2, 8, 128), jnp.float32),
         ),
-        in_specs=[vmem, vmem, smem, smem, smem, smem],
-        out_specs=(vmem, vmem, vmem),
+        in_specs=[pl.BlockSpec(memory_space=pltpu.HBM)] * 6,
+        out_specs=(pl.BlockSpec(memory_space=pltpu.HBM), vmem, vmem),
         scratch_shapes=[
+            pltpu.VMEM(phases.shape, jnp.int32),
+            pltpu.VMEM(grain.shape, jnp.float32),
+            pltpu.SMEM(phase_cond.shape, jnp.float32),
+            pltpu.SMEM(counts.shape, jnp.int32),
+            pltpu.SMEM(current.shape, jnp.float32),
+            pltpu.SMEM(load.shape, jnp.float32),
+            pltpu.SemaphoreType.DMA((ELEMENTS + 4,)),
+            pltpu.VMEM((YC, ZC, 8, 128), jnp.float32),
+            pltpu.VMEM((ELEMENTS, 3, VOX, YZ), jnp.float32),
+            pltpu.SemaphoreType.DMA((ELEMENTS,)),
             pltpu.VMEM((3, 2 * ELEMENTS * VOX, 128), jnp.float32),
             pltpu.VMEM((XC * HALF, 128), jnp.float32),
             pltpu.VMEM((XC, YC, ZC, 8, 128), jnp.float32),
@@ -368,16 +409,16 @@
             pltpu.VMEM((nrow * ncol, 128), jnp.float32),
             pltpu.SemaphoreType.DMA,
             pltpu.SemaphoreType.DMA,
-            pltpu.SemaphoreType.DMA,
         ],
-        compiler_params=pltpu.CompilerParams(collective_id=0, has_side_effects=True, vmem_limit_bytes=40 * 2**20),
+        compiler_params=pltpu.CompilerParams(collective_id=0, has_side_effects=True),
         name="fused",
     )(phases, grain, phase_cond, counts, current, load)
 
 
-def coarse_kernel(ncol, table_ref, tangent_in, states_in, inc_ref, res_ref, tangent_ref, states_ref, out_sems):
-    stores = [pltpu.make_async_copy(states_in.at[0, 0, e], states_ref.at[0, 0, e], out_sems.at[e]) for e in range(ELEMENTS)]
-    for copy in stores:
+def coarse_kernel(ncol, table_ref, tangent_in, states_in, inc_ref, res_ref, tangent_ref, states_ref, held, in_sems, out_sems):
+    loads = [pltpu.make_async_copy(states_in.at[0, 0, e], held.at[e], in_sems.at[e]) for e in range(ELEMENTS)]
+    stores = [pltpu.make_async_copy(held.at[e], states_ref.at[0, 0, e], out_sems.at[e]) for e in range(ELEMENTS)]
+    for copy in loads:
         copy.start()
     tangent_ref[...] = tangent_in[...]
 
@@ -461,6 +502,10 @@
         residual = axpy(-alpha, s, residual)
         if deep is not None:
             image = axpy(-alpha, z, image)
+        if i == 1:
+            for incoming, outgoing in zip(loads, stores):
+                incoming.wait()
+                outgoing.start()
 
     row, col = lax.axis_index("row"), lax.axis_index("col")
     for value, ref in ((increment, inc_ref), (residual, res_ref)):
@@ -488,9 +533,10 @@
         in_specs=[vmem, vmem, anywhere],
         out_specs=(vmem, vmem, vmem, anywhere),
         scratch_shapes=[
+            pltpu.VMEM((ELEMENTS, 3, VOX, YZ), jnp.float32),
+            pltpu.SemaphoreType.DMA((ELEMENTS,)),
             pltpu.SemaphoreType.DMA((ELEMENTS,)),
         ],
-        compiler_params=pltpu.CompilerParams(vmem_limit_bytes=16 * 2**20),
         name="coarse",
     )(table, tangent, states)
 

time: 47.7 us -> 40.6 us (0.85)
  local copies, waits for them, and re-layouts: 4.67 us -> 0 us
  Pallas kernels: 42.1 us -> 39.8 us
    unnamed x12 -> x0, local copies, waits for them, and re-layouts: 4.67 us -> none
    pallas_call x1, Pallas kernels: 39.5 us -> 36.1 us  [fused(): pl.pallas_call(functools.partial(fused_kernel, nrow, ncol), out_shape=(ja...]
    pallas_call x1, Pallas kernels: 2.66 us -> 3.7 us  [coarse(): pl.pallas_call(functools.partial(coarse_kernel, ncol), out_shape=(small,...]
where the time goes in v2:
time: 40.6 us; the launch traced here: 40.4 us
  Pallas kernels  39.8 us (98%)
  between operations  0.64 us (2%)
    pallas_call x1, Pallas kernels, fused(): pl.pallas_call(functools.partial(fused_kernel, nrow, ncol), out_shape=(ja...  36.1 us
    pallas_call x1, Pallas kernels, coarse(): pl.pallas_call(functools.partial(coarse_kernel, ncol), out_shape=(small,...  3.7 us

profile of v2, /device:TPU:1, one launch (start us, length us, event | category | flops | bytes accessed | tf_op | source)
XLA Modules:
  0.0 40.4 jit_solution(2380638838721963094)
XLA Ops:
  0.6 36.1 %fused.1 = (f32[1,1,8,3,24,576]{5,4,3,2,1,0:T(8,128)}, f32[1,3,3,1,8]{4,3,2,1,0:T(1,128)}, f32[5,2,8,128]{3,2,1,0:T(8,128)}) custom-call(s32[1,1,8,24,576]{4,3,2,1,0:T(8,128)} %phases_in.1, f32[1,1,8,24,576]{4,3,2,1,0:T(8,128)} %grain_in.1, f32[3]{0:T(128)} %pc_in.1, s32[1,1,8]{2,1,0:T(1,128)} %counts_in.1, f32[1,1,8]{2,1,0:T(1,128)} %current_in.1, ...), custom_call_target="tpu_custom_call" | custom-call | tf_op jit(solution)/shard_map/fused/pallas_call | solution.py:383
  36.7 3.7 %coarse.1 = (f32[1,1,8]{2,1,0:T(1,128)}, f32[1,1,8]{2,1,0:T(1,128)}, f32[1,3,3,1,8]{4,3,2,1,0:T(1,128)}, f32[1,1,8,3,24,576]{5,4,3,2,1,0:T(8,128)}) custom-call(f32[5,2,8,128]{3,2,1,0:T(8,128)} %get-tuple-element.11.table_ref, f32[1,3,3,1,8]{4,3,2,1,0:T(1,128)} %get-tuple-element.12.tangent_in, f32[1,1,8,3,24,576]{5,4,3,2,1,0:T(8,128)} %get-tuple-element.13.states_in), custom_call_target="tpu_custom_call" | custom-call | tf_op jit(solution)/shard_map/coarse/pallas_call | solution.py:526

commit v3 on v2

--- a/solution.py
+++ b/solution.py
@@ -45,8 +45,13 @@
         value = value + pltpu.roll(value, shift, 0)
     k = lax.broadcasted_iota(jnp.int32, (128, 128), 0)
     j = lax.broadcasted_iota(jnp.int32, (128, 128), 1)
-    same = jnp.where((k & 7) == (j & 7), 1.0, 0.0)
-    return jnp.dot(value, same, precision=lax.Precision.HIGHEST, preferred_element_type=jnp.float32)
+    same = jnp.where((k & 7) == (j & 7), 1.0, 0.0).astype(jnp.bfloat16)
+    first = value.astype(jnp.bfloat16)
+    rest = value - first.astype(jnp.float32)
+    second = rest.astype(jnp.bfloat16)
+    third = (rest - second.astype(jnp.float32)).astype(jnp.bfloat16)
+    parts = [jnp.dot(part, same, preferred_element_type=jnp.float32) for part in (first, second, third)]
+    return parts[0] + (parts[1] + parts[2])
 
 
 SPOTS = [(xc, zc) for xc in range(XC) for zc in range(ZC)]

time: 40.6 us -> 39.7 us (0.978)
  Pallas kernels: 39.8 us -> 38.9 us
    pallas_call x1, Pallas kernels: 36.1 us -> 35.2 us  [fused(): pl.pallas_call(functools.partial(fused_kernel, nrow, ncol), out_shape=(ja...]
where the time goes in v3:
time: 39.7 us; the launch traced here: 39.5 us
  Pallas kernels  38.9 us (98%)
  between operations  0.64 us (2%)
    pallas_call x1, Pallas kernels, fused(): pl.pallas_call(functools.partial(fused_kernel, nrow, ncol), out_shape=(ja...  35.2 us
    pallas_call x1, Pallas kernels, coarse(): pl.pallas_call(functools.partial(coarse_kernel, ncol), out_shape=(small,...  3.7 us

profile of v3, /device:TPU:1, one launch (start us, length us, event | category | flops | bytes accessed | tf_op | source)
XLA Modules:
  0.0 39.5 jit_solution(14400984030478986674)
XLA Ops:
  0.6 35.2 %fused.1 = (f32[1,1,8,3,24,576]{5,4,3,2,1,0:T(8,128)}, f32[1,3,3,1,8]{4,3,2,1,0:T(1,128)}, f32[5,2,8,128]{3,2,1,0:T(8,128)}) custom-call(s32[1,1,8,24,576]{4,3,2,1,0:T(8,128)} %phases_in.1, f32[1,1,8,24,576]{4,3,2,1,0:T(8,128)} %grain_in.1, f32[3]{0:T(128)} %pc_in.1, s32[1,1,8]{2,1,0:T(1,128)} %counts_in.1, f32[1,1,8]{2,1,0:T(1,128)} %current_in.1, ...), custom_call_target="tpu_custom_call" | custom-call | tf_op jit(solution)/shard_map/fused/pallas_call | solution.py:388
  35.8 3.7 %coarse.1 = (f32[1,1,8]{2,1,0:T(1,128)}, f32[1,1,8]{2,1,0:T(1,128)}, f32[1,3,3,1,8]{4,3,2,1,0:T(1,128)}, f32[1,1,8,3,24,576]{5,4,3,2,1,0:T(8,128)}) custom-call(f32[5,2,8,128]{3,2,1,0:T(8,128)} %get-tuple-element.11.table_ref, f32[1,3,3,1,8]{4,3,2,1,0:T(1,128)} %get-tuple-element.12.tangent_in, f32[1,1,8,3,24,576]{5,4,3,2,1,0:T(8,128)} %get-tuple-element.13.states_in), custom_call_target="tpu_custom_call" | custom-call | tf_op jit(solution)/shard_map/coarse/pallas_call | solution.py:531
